TPU v7x, 128 devices: a whole 4x4x4 slice. The times are simulated.
128 devices in a mesh: row: 16 (over x, z), col: 8 (over y, core).
Axes of the slice: x: 4, y: 4, z: 4, core: 2. Of those that a mesh axis runs over, the one named last changes fastest.
Arguments:
- old_params: float32 [2, 256, 32768], P(None, ('row', 'col')), may hold values from -0.12 to 0.12
- old_first: float32 [2, 256, 32768], P(None, ('row', 'col')), may hold values from -1.8 to 1.8
- old_second: float32 [2, 256, 32768], P(None, ('row', 'col')), may hold values from 0.001 to 1
- gradients: float32 [2, 128, 65536], P(None, ('row', 'col')), may hold values from -250 to 250
- old_table: int32 [2, 256], replicated, may hold values from 0 to 255, as said below
- new_table: int32 [2, 128], replicated, may hold values from 0 to 127, as said below
Outputs:
- new_params: float32 [2, 128, 65536], P(None, ('row', 'col'))
- new_first: float32 [2, 128, 65536], P(None, ('row', 'col'))
- new_second: float32 [2, 128, 65536], P(None, ('row', 'col'))
Inputs may be any that keep to these rules, and one draw needn't show every extreme that they name: old_table[t, p] = p XOR k for one k per tensor. new_table[t, q] = q XOR k for one k per tensor.
All inputs are finite; a program needn't handle non-finite values.
Results may differ from a plain program's by a relative error of at most 0.00002.
Values sent between devices are 32-bit elements; how exact they have to be, the bound alone decides.
A program may use at most 64 MiB of HBM per device.

v0:
```python
import math
import jax
import jax.numpy as jnp
from jax import lax
from jax.sharding import Mesh
from jax.sharding import PartitionSpec as P

STEP = 100
ROW_COL = ("row_0", "row_1", "col_0", "col_1")
beta_one = 0.9
beta_two = 0.95
epsilon = 1e-08
learn_rate = 0.001
decay_rate = 0.1


def one_axis_at_a_time(array, axes):
    for axis in axes:
        array = lax.psum(array, axis)
    return array


def from_partner(array, axis, apart):
    return lax.ppermute(array, axis, [(i, i ^ 1 << apart) for i in range(lax.axis_size(axis))])


def adam_update(params, first_moment, second_moment, gradients, clip_factor):
    scaled = clip_factor * gradients
    first_new = beta_one * first_moment + (1.0 - beta_one) * scaled
    second_new = beta_two * second_moment + (1.0 - beta_two) * scaled * scaled
    bias_first = 1.0 - beta_one**STEP
    bias_second = 1.0 - beta_two**STEP
    update = first_new / bias_first / (jnp.sqrt(second_new / bias_second) + epsilon)
    params_new = params - learn_rate * (update + decay_rate * params)
    return (params_new, first_new, second_new)


def global_clip(gradients):
    total_squares = one_axis_at_a_time(jnp.sum(gradients * gradients), ROW_COL)
    count = gradients.size * lax.axis_size(ROW_COL)
    limit = jnp.float32(0.5 * math.sqrt(count))
    return limit / jnp.maximum(jnp.sqrt(total_squares), limit)


def move_state(content, route_key):
    bit_total = lax.axis_size(ROW_COL).bit_length() - 1
    for bit_number in range(bit_total):
        flagged = jnp.bitwise_and(jnp.right_shift(route_key, bit_number), 1) == 1
        needed = jnp.any(flagged)

        def do_swap(state, flagged=flagged, bit_number=bit_number):
            received = from_partner(state, ROW_COL, bit_number)
            return jnp.where(flagged[None, :, None, None], received, state)

        def keep_state(state):
            return state

        content = lax.cond(needed, do_swap, keep_state, content)
    return content


def shards(old_params, old_first, old_second, gradients, old_table, new_table):
    old_key = old_table[:, 0]
    route_key = jnp.bitwise_xor(jnp.right_shift(old_key, 1), new_table[:, 0])
    content = jnp.stack([old_params, old_first, old_second])
    swapped = content[:, :, ::-1, :]
    low_set = jnp.bitwise_and(old_key, 1) == 1
    content = jnp.where(low_set[None, :, None, None], swapped, content)
    content = move_state(content, route_key)
    clip_factor = global_clip(gradients)
    shaped = content.reshape(3, content.shape[1], 1, 2 * content.shape[3])
    return adam_update(shaped[0], shaped[1], shaped[2], gradients, clip_factor)


def solution(mesh):
    finer = Mesh(mesh.devices.reshape(4, 4, 4, 2), ("row_0", "row_1", "col_0", "col_1"))
    in_specs = (
        P(None, ROW_COL, None),
        P(None, ROW_COL, None),
        P(None, ROW_COL, None),
        P(None, ROW_COL, None),
        P(),
        P(),
    )
    out_specs = (P(None, ROW_COL, None), P(None, ROW_COL, None), P(None, ROW_COL, None))
    return jax.shard_map(
        shards, mesh=finer, in_specs=in_specs, out_specs=out_specs, check_vma=False
    )
```

profile of v0, /device:TPU:1, one launch (start us, length us, event | category | flops | bytes accessed | tf_op | source)
XLA Modules:
  0.0 250.2 jit_solution(17393433382442638120)
XLA Ops:
  0.6 2.0 pad_maximum_fusion
  2.7 9.7 %rev.3 = f32[3,2,2,32768]{3,2,1,0:T(2,128)S(1)} reverse(f32[3,2,2,32768]{3,2,1,0:T(2,128)S(1)} %pad_maximum_fusion), dimensions={2} | reverse | bytes 3145728 | tf_op jit(solution)/shard_map/rev | solution.py:66
  13.1 2.2 broadcast_select_fusion.7
  17.4 36.9 %conditional.8 = (f32[3,2,2,32768]{3,2,1,0:T(2,128)S(1)}) conditional(s32[]{:T(128)} %convert_element_type.26, f32[3,2,2,32768]{3,2,1,0:T(2,128)S(1)} %get-tuple-element.112, (pred[2,1]{1,0:T(4,128)(4,1)S(1)}, f32[3,2,2,32768]{3,2,1,0:T(2,128)S(1)}) %tuple.51), branch_computations={%region_9.10_spmd, %region_10.11_spmd} | conditional | flops 393216 | bytes 11010103 | solution.py:58
  17.4 2.2 collective-permute-start.1
  19.7 33.6 %collective-permute-done.1 = f32[3,2,2,32768]{3,2,1,0:T(2,128)S(1)} collective-permute-done((f32[3,2,2,32768]{3,2,1,0:T(2,128)S(1)}, f32[3,2,2,32768]{3,2,1,0:T(2,128)S(1)}, u32[]{:S(2)}, u32[]{:S(2)}) %collective-permute-start.1) | collective-permute-done | bytes 1572896 | tf_op jit(solution)/shard_map/cond/branch_1_fun/ppermute | solution.py:24
  55.0 37.3 %conditional.9 = (f32[3,2,2,32768]{3,2,1,0:T(2,128)S(1)}) conditional(s32[]{:T(128)} %convert_element_type.25, f32[3,2,2,32768]{3,2,1,0:T(2,128)S(1)} %get-tuple-element.113, (pred[2,1]{1,0:T(4,128)(4,1)S(1)}, f32[3,2,2,32768]{3,2,1,0:T(2,128)S(1)}) %tuple.52), branch_computations={%region_11.12_spmd, %region_12.13_spmd} | conditional | flops 393216 | bytes 11010103 | solution.py:58
  55.0 3.2 %collective-permute-start.2 = (f32[3,2,2,32768]{3,2,1,0:T(2,128)S(1)}, f32[3,2,2,32768]{3,2,1,0:T(2,128)S(1)}, u32[]{:S(2)}, u32[]{:S(2)}) collective-permute-start(f32[3,2,2,32768]{3,2,1,0:T(2,128)S(1)} %get-tuple-element.61), channel_id=1, source_target_pairs={{0,4},{1,5},{2,6},{3,7},{4,0},{5,1},{6,2},{7,3},{8,12},{9,13},{10,... | collective-permute-start | bytes 4718600 | tf_op jit(solution)/shard_map/cond/branch_1_fun/ppermute | solution.py:24
  58.4 33.0 %collective-permute-done.2 = f32[3,2,2,32768]{3,2,1,0:T(2,128)S(1)} collective-permute-done((f32[3,2,2,32768]{3,2,1,0:T(2,128)S(1)}, f32[3,2,2,32768]{3,2,1,0:T(2,128)S(1)}, u32[]{:S(2)}, u32[]{:S(2)}) %collective-permute-start.2) | collective-permute-done | bytes 1572896 | tf_op jit(solution)/shard_map/cond/branch_1_fun/ppermute | solution.py:24
  92.9 35.0 %conditional.10 = (f32[3,2,2,32768]{3,2,1,0:T(2,128)S(1)}) conditional(s32[]{:T(128)} %convert_element_type.24, f32[3,2,2,32768]{3,2,1,0:T(2,128)S(1)} %get-tuple-element.114, (pred[2,1]{1,0:T(4,128)(4,1)S(1)}, f32[3,2,2,32768]{3,2,1,0:T(2,128)S(1)}) %tuple.53), branch_computations={%region_13.14_spmd, %region_14.15_spmd} | conditional | flops 393216 | bytes 11010103 | solution.py:58
  93.0 1.7 collective-permute-start.3
  94.7 32.2 %collective-permute-done.3 = f32[3,2,2,32768]{3,2,1,0:T(2,128)S(1)} collective-permute-done((f32[3,2,2,32768]{3,2,1,0:T(2,128)S(1)}, f32[3,2,2,32768]{3,2,1,0:T(2,128)S(1)}, u32[]{:S(2)}, u32[]{:S(2)}) %collective-permute-start.3) | collective-permute-done | bytes 1572896 | tf_op jit(solution)/shard_map/cond/branch_1_fun/ppermute | solution.py:24
  128.6 35.8 %conditional.11 = (f32[3,2,2,32768]{3,2,1,0:T(2,128)S(1)}) conditional(s32[]{:T(128)} %convert_element_type.23, f32[3,2,2,32768]{3,2,1,0:T(2,128)S(1)} %get-tuple-element.115, (pred[2,1]{1,0:T(4,128)(4,1)S(1)}, f32[3,2,2,32768]{3,2,1,0:T(2,128)S(1)}) %tuple.54), branch_computations={%region_15.16_spmd, %region_16.17_spmd} | conditional | flops 393216 | bytes 11010103 | solution.py:58
  128.6 3.3 %collective-permute-start.4 = (f32[3,2,2,32768]{3,2,1,0:T(2,128)S(1)}, f32[3,2,2,32768]{3,2,1,0:T(2,128)S(1)}, u32[]{:S(2)}, u32[]{:S(2)}) collective-permute-start(f32[3,2,2,32768]{3,2,1,0:T(2,128)S(1)} %get-tuple-element.65), channel_id=1, source_target_pairs={{0,16},{1,17},{2,18},{3,19},{4,20},{5,21},{6,22},{7,23},{8,24},{9,... | collective-permute-start | bytes 4718600 | tf_op jit(solution)/shard_map/cond/branch_1_fun/ppermute | solution.py:24
  132.0 31.4 %collective-permute-done.4 = f32[3,2,2,32768]{3,2,1,0:T(2,128)S(1)} collective-permute-done((f32[3,2,2,32768]{3,2,1,0:T(2,128)S(1)}, f32[3,2,2,32768]{3,2,1,0:T(2,128)S(1)}, u32[]{:S(2)}, u32[]{:S(2)}) %collective-permute-start.4) | collective-permute-done | bytes 1572896 | tf_op jit(solution)/shard_map/cond/branch_1_fun/ppermute | solution.py:24
  165.0 33.2 %conditional.12 = (f32[3,2,2,32768]{3,2,1,0:T(2,128)S(1)}) conditional(s32[]{:T(128)} %convert_element_type.22, f32[3,2,2,32768]{3,2,1,0:T(2,128)S(1)} %get-tuple-element.116, (pred[2,1]{1,0:T(4,128)(4,1)S(1)}, f32[3,2,2,32768]{3,2,1,0:T(2,128)S(1)}) %tuple.55), branch_computations={%region_17.18_spmd, %region_18.19_spmd} | conditional | flops 393216 | bytes 11010103 | solution.py:58
  165.0 1.3 collective-permute-start.5
  166.4 30.8 %collective-permute-done.5 = f32[3,2,2,32768]{3,2,1,0:T(2,128)S(1)} collective-permute-done((f32[3,2,2,32768]{3,2,1,0:T(2,128)S(1)}, f32[3,2,2,32768]{3,2,1,0:T(2,128)S(1)}, u32[]{:S(2)}, u32[]{:S(2)}) %collective-permute-start.5) | collective-permute-done | bytes 1572896 | tf_op jit(solution)/shard_map/cond/branch_1_fun/ppermute | solution.py:24
  202.2 1.7 multiply_reduce_fusion
  203.9 9.1 %psum.28 = f32[]{:T(128)} all-reduce(f32[]{:T(128)} %multiply_reduce_fusion), channel_id=1, replica_groups=mesh['row_0'=4,'row_1'=4,'col_0'=4,'col_1'=2] {'row_0'}, use_global_device_ids=true, to_apply=%region_22.23 | all-reduce | flops 1 | bytes 8 | tf_op jit(solution)/shard_map/psum | solution.py:19
  213.0 9.2 %psum.29 = f32[]{:T(128)} all-reduce(f32[]{:T(128)} %psum.28), channel_id=1, replica_groups=mesh['row_0'=4,'row_1'=4,'col_0'=4,'col_1'=2] {'row_1'}, use_global_device_ids=true, to_apply=%region_23.24 | all-reduce | flops 1 | bytes 8 | tf_op jit(solution)/shard_map/psum | solution.py:19
  222.1 9.3 %psum.30 = f32[]{:T(128)} all-reduce(f32[]{:T(128)} %psum.29), channel_id=1, replica_groups=mesh['row_0'=4,'row_1'=4,'col_0'=4,'col_1'=2] {'col_0'}, use_global_device_ids=true, to_apply=%region_24.25 | all-reduce | flops 1 | bytes 8 | tf_op jit(solution)/shard_map/psum | solution.py:19
  231.4 13.7 %psum.31 = f32[]{:T(128)} all-reduce(f32[]{:T(128)} %psum.30), channel_id=1, replica_groups=mesh['row_0'=4,'row_1'=4,'col_0'=4,'col_1'=2] {'col_1'}, use_global_device_ids=true, to_apply=%region_25.26 | all-reduce | flops 1 | bytes 8 | tf_op jit(solution)/shard_map/psum | solution.py:19
  245.9 4.3 %multiply_subtract_fusion = (f32[2,1,65536]{2,1,0:T(1,128)}, f32[2,1,65536]{2,1,0:T(1,128)}, f32[2,1,65536]{2,1,0:T(1,128)}) fusion(f32[2,1,65536]{2,1,0:T(1,128)S(1)} %squeeze.2, f32[2,1,65536]{2,1,0:T(1,128)S(1)} %mul.74, f32[2,1,65536]{2,1,0:T(1,128)S(1)} %copy-done, f32[]{:T(128)S(6)} %div.18, f32[2,1,65536]{2,1,0:T(1,128)S(1)} %mul.81), kind=kLoop, calls=%fused_computation.13 | loop fusion | flops 1835008 | bytes 3670020 | tf_op jit(solution)/shard_map/sub | solution.py:34
  (24 shorter events, 10.2 us)
Async XLA Ops:
  2.7 9.8 %copy-start.1 = (s32[2,128]{1,0:T(2,128)S(1)}, s32[2,128]{1,0:T(2,128)}, u32[]{:S(2)}) copy-start(s32[2,128]{1,0:T(2,128)} %param.25) | copy-start | bytes 3076
  2.7 9.8 %copy-start.2 = (s32[2,256]{1,0:T(2,128)S(1)}, s32[2,256]{1,0:T(2,128)}, u32[]{:S(2)}) copy-start(s32[2,256]{1,0:T(2,128)} %param.24) | copy-start | bytes 6148
  17.4 36.0 %collective-permute-start.1 = (f32[3,2,2,32768]{3,2,1,0:T(2,128)S(1)}, f32[3,2,2,32768]{3,2,1,0:T(2,128)S(1)}, u32[]{:S(2)}, u32[]{:S(2)}) collective-permute-start(f32[3,2,2,32768]{3,2,1,0:T(2,128)S(1)} %get-tuple-element.59), channel_id=1, source_target_pairs={{0,2},{1,3},{2,0},{3,1},{4,6},{5,7},{6,4},{7,5},{8,10},{9,11},{10,... | collective-permute-start | bytes 4718600 | tf_op jit(solution)/shard_map/cond/branch_1_fun/ppermute | solution.py:24
  55.0 36.3 %collective-permute-start.2 = (f32[3,2,2,32768]{3,2,1,0:T(2,128)S(1)}, f32[3,2,2,32768]{3,2,1,0:T(2,128)S(1)}, u32[]{:S(2)}, u32[]{:S(2)}) collective-permute-start(f32[3,2,2,32768]{3,2,1,0:T(2,128)S(1)} %get-tuple-element.61), channel_id=1, source_target_pairs={{0,4},{1,5},{2,6},{3,7},{4,0},{5,1},{6,2},{7,3},{8,12},{9,13},{10,... | collective-permute-start | bytes 4718600 | tf_op jit(solution)/shard_map/cond/branch_1_fun/ppermute | solution.py:24
  93.0 34.0 %collective-permute-start.3 = (f32[3,2,2,32768]{3,2,1,0:T(2,128)S(1)}, f32[3,2,2,32768]{3,2,1,0:T(2,128)S(1)}, u32[]{:S(2)}, u32[]{:S(2)}) collective-permute-start(f32[3,2,2,32768]{3,2,1,0:T(2,128)S(1)} %get-tuple-element.63), channel_id=1, source_target_pairs={{0,8},{1,9},{2,10},{3,11},{4,12},{5,13},{6,14},{7,15},{8,0},{9,1},... | collective-permute-start | bytes 4718600 | tf_op jit(solution)/shard_map/cond/branch_1_fun/ppermute | solution.py:24
  128.6 34.8 %collective-permute-start.4 = (f32[3,2,2,32768]{3,2,1,0:T(2,128)S(1)}, f32[3,2,2,32768]{3,2,1,0:T(2,128)S(1)}, u32[]{:S(2)}, u32[]{:S(2)}) collective-permute-start(f32[3,2,2,32768]{3,2,1,0:T(2,128)S(1)} %get-tuple-element.65), channel_id=1, source_target_pairs={{0,16},{1,17},{2,18},{3,19},{4,20},{5,21},{6,22},{7,23},{8,24},{9,... | collective-permute-start | bytes 4718600 | tf_op jit(solution)/shard_map/cond/branch_1_fun/ppermute | solution.py:24
  165.0 32.2 %collective-permute-start.5 = (f32[3,2,2,32768]{3,2,1,0:T(2,128)S(1)}, f32[3,2,2,32768]{3,2,1,0:T(2,128)S(1)}, u32[]{:S(2)}, u32[]{:S(2)}) collective-permute-start(f32[3,2,2,32768]{3,2,1,0:T(2,128)S(1)} %get-tuple-element.67), channel_id=1, source_target_pairs={{0,32},{1,33},{2,34},{3,35},{4,36},{5,37},{6,38},{7,39},{8,40},{9,... | collective-permute-start | bytes 4718600 | tf_op jit(solution)/shard_map/cond/branch_1_fun/ppermute | solution.py:24
  199.6 2.6 %copy-start = (f32[2,1,65536]{2,1,0:T(1,128)S(1)}, f32[2,1,65536]{2,1,0:T(1,128)}, u32[]{:S(2)}) copy-start(f32[2,1,65536]{2,1,0:T(1,128)} %param.23) | copy-start | bytes 1572868
where the time goes:
time: 250 us
  waiting for transfers between devices  161 us (64%)
  blocking collectives  41.3 us (17%)
  other arithmetic  17.6 us (7%)
  local copies, waits for them, and re-layouts  12.3 us (5%)
  starting transfers between devices  11.6 us (5%)
  between operations  5.99 us (2%)
    ppermute x5, waiting for transfers between devices, from_partner(): lax.ppermute(array, axis, [(i, i ^ 1 << apart) for i in range(lax.axis_si...  161 us
    psum x4, blocking collectives, one_axis_at_a_time(): array = lax.psum(array, axis)  41.3 us
    ppermute x5, starting transfers between devices, from_partner(): lax.ppermute(array, axis, [(i, i ^ 1 << apart) for i in range(lax.axis_si...  11.6 us
    rev x1, local copies, waits for them, and re-layouts, shards(): swapped = content[:, :, ::-1, :]  9.74 us
  transfers between devices with their start and end apart: 5, of which 5 were waited for; matrix products, arithmetic and copies ran while one was open for 0% of the time, Pallas kernels for 0%

commit v1 on v0

--- a/solution.py
+++ b/solution.py
@@ -16,7 +16,7 @@
 
 def one_axis_at_a_time(array, axes):
     for axis in axes:
-        array = lax.psum(array, axis)
+        array = jnp.sum(lax.all_gather(array, axis), axis=0)
     return array
 
 

time: 250 us -> 258 us (1.032)
  local copies, waits for them, and re-layouts: 12.3 us -> 20.3 us
    psum x4 -> x0, blocking collectives: 41.3 us -> none  [one_axis_at_a_time(): array = lax.psum(array, axis)]
    unnamed x0 -> x4, blocking collectives: none -> 38.8 us
    unnamed x6 -> x26, local copies, waits for them, and re-layouts: 0.02 us -> 7.99 us
where the time goes in v1:
time: 258 us
  waiting for transfers between devices  161 us (62%)
  blocking collectives  38.8 us (15%)
  local copies, waits for them, and re-layouts  20.3 us (8%)
  other arithmetic  20 us (8%)
  starting transfers between devices  11.6 us (4%)
  between operations  6.04 us (2%)
    ppermute x5, waiting for transfers between devices, from_partner(): lax.ppermute(array, axis, [(i, i ^ 1 << apart) for i in range(lax.axis_si...  161 us
    unnamed x4, blocking collectives  38.8 us
    ppermute x5, starting transfers between devices, from_partner(): lax.ppermute(array, axis, [(i, i ^ 1 << apart) for i in range(lax.axis_si...  11.6 us
    rev x1, local copies, waits for them, and re-layouts, shards(): swapped = content[:, :, ::-1, :]  9.74 us
    unnamed x26, local copies, waits for them, and re-layouts  7.99 us
  transfers between devices with their start and end apart: 5, of which 5 were waited for; matrix products, arithmetic and copies ran while one was open for 0% of the time, Pallas kernels for 0%

profile of v1, /device:TPU:1, one launch (start us, length us, event | category | flops | bytes accessed | tf_op | source)
XLA Modules:
  0.0 258.1 jit_solution(4898382784335298163)
XLA Ops:
  0.6 2.0 pad_maximum_fusion
  2.7 9.7 %rev.3 = f32[3,2,2,32768]{3,2,1,0:T(2,128)S(1)} reverse(f32[3,2,2,32768]{3,2,1,0:T(2,128)S(1)} %pad_maximum_fusion), dimensions={2} | reverse | bytes 3145728 | tf_op jit(solution)/shard_map/rev | solution.py:66
  13.1 2.2 broadcast_select_fusion.7
  17.4 36.9 %conditional.8 = (f32[3,2,2,32768]{3,2,1,0:T(2,128)S(1)}) conditional(s32[]{:T(128)} %convert_element_type.26, f32[3,2,2,32768]{3,2,1,0:T(2,128)S(1)} %get-tuple-element.112, (pred[2,1]{1,0:T(4,128)(4,1)S(1)}, f32[3,2,2,32768]{3,2,1,0:T(2,128)S(1)}) %tuple.51), branch_computations={%region_9.10_spmd, %region_10.11_spmd} | conditional | flops 393216 | bytes 11010103 | solution.py:58
  17.4 2.2 collective-permute-start.1
  19.7 33.6 %collective-permute-done.1 = f32[3,2,2,32768]{3,2,1,0:T(2,128)S(1)} collective-permute-done((f32[3,2,2,32768]{3,2,1,0:T(2,128)S(1)}, f32[3,2,2,32768]{3,2,1,0:T(2,128)S(1)}, u32[]{:S(2)}, u32[]{:S(2)}) %collective-permute-start.1) | collective-permute-done | bytes 1572896 | tf_op jit(solution)/shard_map/cond/branch_1_fun/ppermute | solution.py:24
  55.0 37.3 %conditional.9 = (f32[3,2,2,32768]{3,2,1,0:T(2,128)S(1)}) conditional(s32[]{:T(128)} %convert_element_type.25, f32[3,2,2,32768]{3,2,1,0:T(2,128)S(1)} %get-tuple-element.113, (pred[2,1]{1,0:T(4,128)(4,1)S(1)}, f32[3,2,2,32768]{3,2,1,0:T(2,128)S(1)}) %tuple.52), branch_computations={%region_11.12_spmd, %region_12.13_spmd} | conditional | flops 393216 | bytes 11010103 | solution.py:58
  55.0 3.2 %collective-permute-start.2 = (f32[3,2,2,32768]{3,2,1,0:T(2,128)S(1)}, f32[3,2,2,32768]{3,2,1,0:T(2,128)S(1)}, u32[]{:S(2)}, u32[]{:S(2)}) collective-permute-start(f32[3,2,2,32768]{3,2,1,0:T(2,128)S(1)} %get-tuple-element.61), channel_id=1, source_target_pairs={{0,4},{1,5},{2,6},{3,7},{4,0},{5,1},{6,2},{7,3},{8,12},{9,13},{10,... | collective-permute-start | bytes 4718600 | tf_op jit(solution)/shard_map/cond/branch_1_fun/ppermute | solution.py:24
  58.4 33.0 %collective-permute-done.2 = f32[3,2,2,32768]{3,2,1,0:T(2,128)S(1)} collective-permute-done((f32[3,2,2,32768]{3,2,1,0:T(2,128)S(1)}, f32[3,2,2,32768]{3,2,1,0:T(2,128)S(1)}, u32[]{:S(2)}, u32[]{:S(2)}) %collective-permute-start.2) | collective-permute-done | bytes 1572896 | tf_op jit(solution)/shard_map/cond/branch_1_fun/ppermute | solution.py:24
  92.9 35.0 %conditional.10 = (f32[3,2,2,32768]{3,2,1,0:T(2,128)S(1)}) conditional(s32[]{:T(128)} %convert_element_type.24, f32[3,2,2,32768]{3,2,1,0:T(2,128)S(1)} %get-tuple-element.114, (pred[2,1]{1,0:T(4,128)(4,1)S(1)}, f32[3,2,2,32768]{3,2,1,0:T(2,128)S(1)}) %tuple.53), branch_computations={%region_13.14_spmd, %region_14.15_spmd} | conditional | flops 393216 | bytes 11010103 | solution.py:58
  93.0 1.7 collective-permute-start.3
  94.7 32.2 %collective-permute-done.3 = f32[3,2,2,32768]{3,2,1,0:T(2,128)S(1)} collective-permute-done((f32[3,2,2,32768]{3,2,1,0:T(2,128)S(1)}, f32[3,2,2,32768]{3,2,1,0:T(2,128)S(1)}, u32[]{:S(2)}, u32[]{:S(2)}) %collective-permute-start.3) | collective-permute-done | bytes 1572896 | tf_op jit(solution)/shard_map/cond/branch_1_fun/ppermute | solution.py:24
  128.6 35.8 %conditional.11 = (f32[3,2,2,32768]{3,2,1,0:T(2,128)S(1)}) conditional(s32[]{:T(128)} %convert_element_type.23, f32[3,2,2,32768]{3,2,1,0:T(2,128)S(1)} %get-tuple-element.115, (pred[2,1]{1,0:T(4,128)(4,1)S(1)}, f32[3,2,2,32768]{3,2,1,0:T(2,128)S(1)}) %tuple.54), branch_computations={%region_15.16_spmd, %region_16.17_spmd} | conditional | flops 393216 | bytes 11010103 | solution.py:58
  128.6 3.3 %collective-permute-start.4 = (f32[3,2,2,32768]{3,2,1,0:T(2,128)S(1)}, f32[3,2,2,32768]{3,2,1,0:T(2,128)S(1)}, u32[]{:S(2)}, u32[]{:S(2)}) collective-permute-start(f32[3,2,2,32768]{3,2,1,0:T(2,128)S(1)} %get-tuple-element.65), channel_id=1, source_target_pairs={{0,16},{1,17},{2,18},{3,19},{4,20},{5,21},{6,22},{7,23},{8,24},{9,... | collective-permute-start | bytes 4718600 | tf_op jit(solution)/shard_map/cond/branch_1_fun/ppermute | solution.py:24
  132.0 31.4 %collective-permute-done.4 = f32[3,2,2,32768]{3,2,1,0:T(2,128)S(1)} collective-permute-done((f32[3,2,2,32768]{3,2,1,0:T(2,128)S(1)}, f32[3,2,2,32768]{3,2,1,0:T(2,128)S(1)}, u32[]{:S(2)}, u32[]{:S(2)}) %collective-permute-start.4) | collective-permute-done | bytes 1572896 | tf_op jit(solution)/shard_map/cond/branch_1_fun/ppermute | solution.py:24
  165.0 33.2 %conditional.12 = (f32[3,2,2,32768]{3,2,1,0:T(2,128)S(1)}) conditional(s32[]{:T(128)} %convert_element_type.22, f32[3,2,2,32768]{3,2,1,0:T(2,128)S(1)} %get-tuple-element.116, (pred[2,1]{1,0:T(4,128)(4,1)S(1)}, f32[3,2,2,32768]{3,2,1,0:T(2,128)S(1)}) %tuple.55), branch_computations={%region_17.18_spmd, %region_18.19_spmd} | conditional | flops 393216 | bytes 11010103 | solution.py:58
  166.4 30.8 %collective-permute-done.5 = f32[3,2,2,32768]{3,2,1,0:T(2,128)S(1)} collective-permute-done((f32[3,2,2,32768]{3,2,1,0:T(2,128)S(1)}, f32[3,2,2,32768]{3,2,1,0:T(2,128)S(1)}, u32[]{:S(2)}, u32[]{:S(2)}) %collective-permute-start.5) | collective-permute-done | bytes 1572896 | tf_op jit(solution)/shard_map/cond/branch_1_fun/ppermute | solution.py:24
  202.8 1.7 multiply_reduce_fusion
  204.5 1.4 dynamic-update-slice
  205.9 8.4 %all-reduce = f32[4]{0:T(128)S(1)} all-reduce(f32[4]{0:T(128)S(1)} %dynamic-update-slice), channel_id=1, replica_groups=mesh['row_0'=4,'row_1'=4,'col_0'=4,'col_1'=2] {'row_0'}, use_global_device_ids=true, to_apply=%add | all-reduce | flops 4 | bytes 32
  217.0 8.5 %all-reduce.1 = f32[4]{0:T(128)S(1)} all-reduce(f32[4]{0:T(128)S(1)} %dynamic-update-slice.1), channel_id=1, replica_groups=mesh['row_0'=4,'row_1'=4,'col_0'=4,'col_1'=2] {'row_1'}, use_global_device_ids=true, to_apply=%add.1 | all-reduce | flops 4 | bytes 32
  228.1 8.7 %all-reduce.2 = f32[4]{0:T(128)S(1)} all-reduce(f32[4]{0:T(128)S(1)} %dynamic-update-slice.2), channel_id=1, replica_groups=mesh['row_0'=4,'row_1'=4,'col_0'=4,'col_1'=2] {'col_0'}, use_global_device_ids=true, to_apply=%add.2 | all-reduce | flops 4 | bytes 32
  239.4 13.1 %all-reduce.3 = f32[2]{0:T(128)S(1)} all-reduce(f32[2]{0:T(128)S(1)} %dynamic-update-slice.3), channel_id=1, replica_groups=mesh['row_0'=4,'row_1'=4,'col_0'=4,'col_1'=2] {'col_1'}, use_global_device_ids=true, to_apply=%add.3 | all-reduce | flops 2 | bytes 16
  253.8 4.3 %multiply_subtract_fusion = (f32[2,1,65536]{2,1,0:T(1,128)}, f32[2,1,65536]{2,1,0:T(1,128)}, f32[2,1,65536]{2,1,0:T(1,128)}) fusion(f32[2,1,65536]{2,1,0:T(1,128)S(1)} %squeeze.2, f32[2,1,65536]{2,1,0:T(1,128)S(1)} %mul.74, f32[2,1,65536]{2,1,0:T(1,128)S(1)} %copy-done, f32[]{:T(128)S(6)} %div.18, f32[2,1,65536]{2,1,0:T(1,128)S(1)} %mul.81), kind=kLoop, calls=%fused_computation.13 | loop fusion | flops 1835008 | bytes 3670020 | tf_op jit(solution)/shard_map/sub | solution.py:34
  (48 shorter events, 20.5 us)
Async XLA Ops:
  2.7 9.8 %copy-start.1 = (s32[2,128]{1,0:T(2,128)S(1)}, s32[2,128]{1,0:T(2,128)}, u32[]{:S(2)}) copy-start(s32[2,128]{1,0:T(2,128)} %param.25) | copy-start | bytes 3076
  2.7 9.8 %copy-start.2 = (s32[2,256]{1,0:T(2,128)S(1)}, s32[2,256]{1,0:T(2,128)}, u32[]{:S(2)}) copy-start(s32[2,256]{1,0:T(2,128)} %param.24) | copy-start | bytes 6148
  17.4 36.0 %collective-permute-start.1 = (f32[3,2,2,32768]{3,2,1,0:T(2,128)S(1)}, f32[3,2,2,32768]{3,2,1,0:T(2,128)S(1)}, u32[]{:S(2)}, u32[]{:S(2)}) collective-permute-start(f32[3,2,2,32768]{3,2,1,0:T(2,128)S(1)} %get-tuple-element.59), channel_id=1, source_target_pairs={{0,2},{1,3},{2,0},{3,1},{4,6},{5,7},{6,4},{7,5},{8,10},{9,11},{10,... | collective-permute-start | bytes 4718600 | tf_op jit(solution)/shard_map/cond/branch_1_fun/ppermute | solution.py:24
  55.0 36.3 %collective-permute-start.2 = (f32[3,2,2,32768]{3,2,1,0:T(2,128)S(1)}, f32[3,2,2,32768]{3,2,1,0:T(2,128)S(1)}, u32[]{:S(2)}, u32[]{:S(2)}) collective-permute-start(f32[3,2,2,32768]{3,2,1,0:T(2,128)S(1)} %get-tuple-element.61), channel_id=1, source_target_pairs={{0,4},{1,5},{2,6},{3,7},{4,0},{5,1},{6,2},{7,3},{8,12},{9,13},{10,... | collective-permute-start | bytes 4718600 | tf_op jit(solution)/shard_map/cond/branch_1_fun/ppermute | solution.py:24
  93.0 34.0 %collective-permute-start.3 = (f32[3,2,2,32768]{3,2,1,0:T(2,128)S(1)}, f32[3,2,2,32768]{3,2,1,0:T(2,128)S(1)}, u32[]{:S(2)}, u32[]{:S(2)}) collective-permute-start(f32[3,2,2,32768]{3,2,1,0:T(2,128)S(1)} %get-tuple-element.63), channel_id=1, source_target_pairs={{0,8},{1,9},{2,10},{3,11},{4,12},{5,13},{6,14},{7,15},{8,0},{9,1},... | collective-permute-start | bytes 4718600 | tf_op jit(solution)/shard_map/cond/branch_1_fun/ppermute | solution.py:24
  128.6 34.8 %collective-permute-start.4 = (f32[3,2,2,32768]{3,2,1,0:T(2,128)S(1)}, f32[3,2,2,32768]{3,2,1,0:T(2,128)S(1)}, u32[]{:S(2)}, u32[]{:S(2)}) collective-permute-start(f32[3,2,2,32768]{3,2,1,0:T(2,128)S(1)} %get-tuple-element.65), channel_id=1, source_target_pairs={{0,16},{1,17},{2,18},{3,19},{4,20},{5,21},{6,22},{7,23},{8,24},{9,... | collective-permute-start | bytes 4718600 | tf_op jit(solution)/shard_map/cond/branch_1_fun/ppermute | solution.py:24
  165.0 32.2 %collective-permute-start.5 = (f32[3,2,2,32768]{3,2,1,0:T(2,128)S(1)}, f32[3,2,2,32768]{3,2,1,0:T(2,128)S(1)}, u32[]{:S(2)}, u32[]{:S(2)}) collective-permute-start(f32[3,2,2,32768]{3,2,1,0:T(2,128)S(1)} %get-tuple-element.67), channel_id=1, source_target_pairs={{0,32},{1,33},{2,34},{3,35},{4,36},{5,37},{6,38},{7,39},{8,40},{9,... | collective-permute-start | bytes 4718600 | tf_op jit(solution)/shard_map/cond/branch_1_fun/ppermute | solution.py:24
  199.6 2.7 %copy-start.6 = (u32[128]{0:T(128)S(1)}, u32[128]{0:T(128)}, u32[]{:S(2)}) copy-start(u32[128]{0:T(128)} %constant.44) | copy-start | bytes 1540
  199.6 3.2 %copy-start = (f32[2,1,65536]{2,1,0:T(1,128)S(1)}, f32[2,1,65536]{2,1,0:T(1,128)}, u32[]{:S(2)}) copy-start(f32[2,1,65536]{2,1,0:T(1,128)} %param.23) | copy-start | bytes 1572868
  200.5 14.5 %copy-start.5 = (u32[128]{0:T(128)S(1)}, u32[128]{0:T(128)}, u32[]{:S(2)}) copy-start(u32[128]{0:T(128)} %constant.49) | copy-start | bytes 1540
  200.5 25.6 %copy-start.4 = (u32[128]{0:T(128)S(1)}, u32[128]{0:T(128)}, u32[]{:S(2)}) copy-start(u32[128]{0:T(128)} %constant.54) | copy-start | bytes 1540
  200.5 36.9 %copy-start.3 = (u32[128]{0:T(128)S(1)}, u32[128]{0:T(128)}, u32[]{:S(2)}) copy-start(u32[128]{0:T(128)} %constant.59) | copy-start | bytes 1540
